TPU v7x, 32 devices: a whole 2x2x4 slice. The times are simulated.
32 devices in a mesh: gx: 4 (over y, core), gy: 8 (over z, x).
Axes of the slice: x: 2, y: 2, z: 4, core: 2. Of those that a mesh axis runs over, the one named last changes fastest.
Arguments:
- pool_old: float32 [40, 131072], P(None, ('gx', 'gy')), may hold values from 0.5 to 2
- pool_new: float32 [40, 131072], P(None, ('gx', 'gy')), may hold values from 0.5 to 2
- flux: float32 [40, 131072], P(None, ('gx', 'gy')), may hold values from -6 to 6
- area: float32 [131072], P(('gx', 'gy')), may hold values from 0.05 to 1
- pft_id: int32 [131072], P(('gx', 'gy')), may hold values from 0 to 78
- region_id: int32 [131072], P(('gx', 'gy')), may hold values from 0 to 31, as said below
Outputs:
- pool_totals: float32 [40, 2528], replicated
- error_totals: float32 [40, 2528], replicated
Inputs may be any that keep to these rules, and one draw needn't show every extreme that they name: `region_id`: patch i lies in block k = i // 4096; with K = 32 blocks, its region is (k * 32) // K or ((k * 32) // K + 1) mod 32.
All inputs are finite; a program needn't handle non-finite values.
Results may differ from a plain program's by a relative error of at most 0.000076.
Values sent between devices are 32-bit elements; how exact they have to be, the bound alone decides.
A program may use at most 64 MiB of HBM per device.

v0:
```python
import jax
import jax.numpy as jnp
from jax import lax
from jax.sharding import PartitionSpec as P

POOLS = 40
PFT = 79
REGION = 32
CELLS = 2528


def shards(pool_old, pool_new, flux, area, pft_id, region_id):
    width_x = lax.axis_size("gx")
    width_y = lax.axis_size("gy")
    devices_all = width_x * width_y
    position = lax.axis_index("gx") * width_y + lax.axis_index("gy")
    base = position * REGION // devices_all
    offset_here = (region_id - base) % REGION
    compact_cell = pft_id * 2 + offset_here
    stored = area[None, :] * pool_new
    balance = area[None, :] * (pool_new - pool_old - 0.5 * flux)
    stacked = jnp.concatenate([stored, balance], axis=0)
    rows = stacked.shape[0]
    patch_count = stacked.shape[1]
    block = min(512, patch_count)
    blocks = patch_count // block
    stacked_blocks = stacked.reshape(rows, blocks, block).transpose(1, 0, 2)
    cell_blocks = compact_cell.reshape(blocks, block)
    columns = jnp.arange(2 * PFT, dtype=jnp.int32)

    def accumulate(totals, inputs):
        values, cells_here = inputs
        onehot = (cells_here[:, None] == columns[None, :]).astype(jnp.float32)
        added = jnp.dot(
            values, onehot, preferred_element_type=jnp.float32, precision=lax.Precision.HIGHEST
        )
        return (totals + added, None)

    local_table, _ = lax.scan(
        accumulate, jnp.zeros((rows, 2 * PFT), jnp.float32), (stacked_blocks, cell_blocks)
    )
    local_table = local_table.reshape(rows, PFT, 2)
    region_axis = jnp.arange(REGION, dtype=jnp.int32)
    pair_axis = jnp.arange(2, dtype=jnp.int32)
    span = REGION // width_x + 1
    start = lax.axis_index("gx") * (REGION // width_x)
    span_axis = jnp.arange(span, dtype=jnp.int32)
    into_group = ((base - start + pair_axis)[:, None] == span_axis[None, :]).astype(jnp.float32)
    group_table = jnp.einsum(
        "apj,jw->apw", local_table, into_group, precision=lax.Precision.HIGHEST
    )
    group_total = lax.psum(group_table, "gy")
    into_full = (((start + span_axis) % REGION)[:, None] == region_axis[None, :]).astype(
        jnp.float32
    )
    placed = jnp.einsum("apw,wr->apr", group_total, into_full, precision=lax.Precision.HIGHEST)
    totals = lax.psum(placed.reshape(rows, CELLS), "gx")
    patch_all = patch_count * devices_all
    totals = totals * jnp.float32(CELLS / patch_all)
    return (totals[:POOLS], totals[POOLS:])


def solution(mesh):
    return jax.shard_map(
        shards,
        mesh=mesh,
        in_specs=(
            P(None, ("gx", "gy")),
            P(None, ("gx", "gy")),
            P(None, ("gx", "gy")),
            P(("gx", "gy")),
            P(("gx", "gy")),
            P(("gx", "gy")),
        ),
        out_specs=(P(), P()),
        check_vma=False,
    )
```

profile of v0, /device:TPU:0, one launch (start us, length us, event | category | flops | bytes accessed | tf_op | source)
XLA Modules:
  0.0 140.4 jit_solution(4403642553132659175)
XLA Ops:
  7.2 0.0 all-reduce.3.cloned.1.call-start
  7.2 0.8 fusion.4
  8.0 1.6 %broadcast_multiply_fusion.1 = (f32[40,4096]{1,0:T(8,128)S(1)}, f32[40,4096]{1,0:T(8,128)S(1)}) fusion(f32[40,4096]{1,0:T(8,128)} %param.9, f32[4096]{0:T(1024)} %param.11, f32[40,4096]{1,0:T(8,128)} %param.10, f32[40,4096]{1,0:T(8,128)} %param.8), kind=kLoop, calls=%fused_computation.10 | loop fusion | flops 819200 | bytes 3293184 | tf_op jit(solution)/shard_map/mul | solution.py:20
  9.6 0.1 pad_maximum_fusion
  9.7 0.8 copy.13
  10.6 4.8 %while.11 = (s32[]{:T(128)}, f32[80,158]{1,0:T(8,128)S(1)}, f32[8,80,512]{2,0,1:T(8,128)S(1)}, s32[8,512]{1,0:T(8,128)S(1)}, s32[]{:T(128)}, /*index=5*/s32[]{:T(128)}) while((s32[]{:T(128)}, f32[80,158]{1,0:T(8,128)S(1)}, f32[8,80,512]{2,0,1:T(8,128)S(1)}, s32[8,512]{1,0:T(8,128)S(1)}, s32[]{:T(128)}, /*index=5*/s32[]{:T(128)}) %tuple.36), condition=%wide.region_1.2_spmd.clone, body=%wide.region_0.1_spmd.clone.sunk | while | flops 77766336 | bytes 598871 | solution.py:39
  10.6 0.1 constant_dynamic-slice_fusion.5
  10.8 0.4 convolution_add_fusion.2
  11.2 0.1 constant_dynamic-slice_fusion.5
  11.4 0.4 convolution_add_fusion.2
  11.8 0.1 constant_dynamic-slice_fusion.5
  12.0 0.4 convolution_add_fusion.2
  12.4 0.1 constant_dynamic-slice_fusion.5
  12.5 0.4 convolution_add_fusion.2
  13.0 0.1 constant_dynamic-slice_fusion.5
  13.1 0.4 convolution_add_fusion.2
  13.6 0.1 constant_dynamic-slice_fusion.5
  13.7 0.4 convolution_add_fusion.2
  14.2 0.1 constant_dynamic-slice_fusion.5
  14.3 0.4 convolution_add_fusion.2
  14.8 0.1 constant_dynamic-slice_fusion.5
  14.9 0.4 convolution_add_fusion.2
  15.3 0.1 copy.10
  15.5 1.4 fusion.9
  16.9 0.0 all-reduce.5.cloned.1.call-start
  17.0 76.4 %all-reduce.3.cloned.1.call-done = f32[80,79,9]{0,2,1:T(8,128)} async-done(((f32[80,79,9]{0,2,1:T(8,128)}), f32[80,79,9]{0,2,1:T(8,128)}) %all-reduce.3.cloned.1.call-update) | async-done | bytes 227536 | tf_op jit(solution)/shard_map/psum | solution.py:52
  93.4 1.9 %fusion.6 = f32[80,79,32]{0,2,1:T(8,128)S(1)} fusion(f32[80,79,9]{0,2,1:T(8,128)} %all-reduce.3.cloned.1.call-done, s32[9]{0:T(128)S(1)} %and_select_fusion), kind=kOutput, calls=%fused_computation.18 | convolution fusion | flops 21842208 | bytes 1036516 | tf_op jit(solution)/shard_map/apw,wr->apr/dot_general | solution.py:56
  95.3 1.3 copy.11
  96.6 0.0 all-reduce.5.cloned.1.call-update
  96.6 34.8 %all-reduce.5.cloned.1.call-done = f32[80,2528]{1,0:T(8,128)} async-done(((f32[80,2528]{1,0:T(8,128)}), f32[80,2528]{1,0:T(8,128)}) %all-reduce.5.cloned.1.call-update) | async-done | bytes 808976 | tf_op jit(solution)/shard_map/psum | solution.py:57
  131.4 1.2 broadcast_multiply_fusion
  132.7 0.9 fusion.15
  (14 shorter events, 0.2 us)
Async XLA Ops:
  7.2 86.3 %all-reduce.3.cloned.1.call-start = ((), (), s32[]{:S(2)}) async-start(), calls=%async_computation | async-start | bytes 1294336 | tf_op jit(solution)/shard_map/psum | solution.py:52
  16.9 114.5 %all-reduce.5.cloned.1.call-start = ((), (), s32[]{:S(2)}) async-start(), calls=%async_computation.1 | async-start | bytes 1638400 | tf_op jit(solution)/shard_map/psum | solution.py:57
Sparse Core Ops, SparseCore 0:
  17.0 76.3 all-reduce.2
  96.7 34.6 all-reduce.4
where the time goes:
time: 141 us; the launch traced here: 140 us
  waiting for transfers between devices  111 us (79%)
  between operations  14.1 us (10%)
  matrix products  6.42 us (5%)
  local copies, waits for them, and re-layouts  4.48 us (3%)
  other arithmetic  3.68 us (3%)
    psum x1, waiting for transfers between devices, shards(): group_total = lax.psum(group_table, 'gy')  76.4 us
    psum x1, waiting for transfers between devices, shards(): totals = lax.psum(placed.reshape(rows, CELLS), 'gx')  34.8 us
    dot_general x8, matrix products, accumulate(): jnp.dot(values, onehot, preferred_element_type=jnp.float32, precision=lax...  3.17 us
  transfers between devices with their start and end apart: 2, of which 2 were waited for; matrix products, arithmetic and copies ran while one was open for 0% of the time, Pallas kernels for 0%

commit v1 on v0

--- a/solution.py
+++ b/solution.py
@@ -49,7 +49,7 @@
     group_table = jnp.einsum(
         "apj,jw->apw", local_table, into_group, precision=lax.Precision.HIGHEST
     )
-    group_total = lax.psum(group_table, "gy")
+    group_total = jnp.sum(lax.all_gather(group_table, "gy"), axis=0)
     into_full = (((start + span_axis) % REGION)[:, None] == region_axis[None, :]).astype(
         jnp.float32
     )

time: 141 us -> 126 us (0.89)
  waiting for transfers between devices: 111 us -> 94.8 us
  other arithmetic: 3.68 us -> 5.75 us
  matrix products: 6.42 us -> 4.51 us
    psum x1 -> x0, waiting for transfers between devices: 76.4 us -> none  [shards(): group_total = lax.psum(group_table, 'gy')]
    all_gather x0 -> x1, waiting for transfers between devices: none -> 60.7 us  [shards(): group_total = jnp.sum(lax.all_gather(group_table, 'gy'), axis=0)]
    reduce_sum x0 -> x1, other arithmetic: none -> 2.07 us  [shards(): group_total = jnp.sum(lax.all_gather(group_table, 'gy'), axis=0)]
where the time goes in v1:
time: 126 us; the launch traced here: 125 us
  waiting for transfers between devices  94.8 us (75%)
  between operations  14.2 us (11%)
  local copies, waits for them, and re-layouts  5.81 us (5%)
  other arithmetic  5.75 us (5%)
  matrix products  4.51 us (4%)
    all_gather x1, waiting for transfers between devices, shards(): group_total = jnp.sum(lax.all_gather(group_table, 'gy'), axis=0)  60.7 us
    psum x1, waiting for transfers between devices, shards(): totals = lax.psum(placed.reshape(rows, CELLS), 'gx')  34 us
    dot_general x8, matrix products, accumulate(): jnp.dot(values, onehot, preferred_element_type=jnp.float32, precision=lax...  3.17 us
  transfers between devices with their start and end apart: 2, of which 2 were waited for; matrix products, arithmetic and copies ran while one was open for 0% of the time, Pallas kernels for 0%

profile of v1, /device:TPU:0, one launch (start us, length us, event | category | flops | bytes accessed | tf_op | source)
XLA Modules:
  0.0 125.4 jit_solution(14067169427104414805)
XLA Ops:
  7.3 0.8 fusion.4
  8.0 1.6 %broadcast_multiply_fusion.1 = (f32[40,4096]{1,0:T(8,128)S(1)}, f32[40,4096]{1,0:T(8,128)S(1)}) fusion(f32[40,4096]{1,0:T(8,128)} %param.9, f32[4096]{0:T(1024)} %param.11, f32[40,4096]{1,0:T(8,128)} %param.10, f32[40,4096]{1,0:T(8,128)} %param.8), kind=kLoop, calls=%fused_computation.10 | loop fusion | flops 819200 | bytes 3293184 | tf_op jit(solution)/shard_map/mul | solution.py:20
  9.6 0.1 pad_maximum_fusion
  9.7 0.8 copy.24
  10.6 4.7 %while.11 = (s32[]{:T(128)}, f32[80,158]{1,0:T(8,128)S(1)}, f32[8,80,512]{2,0,1:T(8,128)S(1)}, s32[8,512]{1,0:T(8,128)S(1)}, s32[]{:T(128)}, /*index=5*/s32[]{:T(128)}) while((s32[]{:T(128)}, f32[80,158]{1,0:T(8,128)S(1)}, f32[8,80,512]{2,0,1:T(8,128)S(1)}, s32[8,512]{1,0:T(8,128)S(1)}, s32[]{:T(128)}, /*index=5*/s32[]{:T(128)}) %tuple.37), condition=%wide.region_1.2_spmd.clone, body=%wide.region_0.1_spmd.clone.sunk | while | flops 77766336 | bytes 598879 | solution.py:39
  10.6 0.1 constant_dynamic-slice_fusion.5
  10.8 0.4 convolution_add_fusion.2
  11.2 0.1 constant_dynamic-slice_fusion.5
  11.4 0.4 convolution_add_fusion.2
  11.8 0.1 constant_dynamic-slice_fusion.5
  12.0 0.4 convolution_add_fusion.2
  12.4 0.1 constant_dynamic-slice_fusion.5
  12.5 0.4 convolution_add_fusion.2
  13.0 0.1 constant_dynamic-slice_fusion.5
  13.1 0.4 convolution_add_fusion.2
  13.6 0.1 constant_dynamic-slice_fusion.5
  13.7 0.4 convolution_add_fusion.2
  14.2 0.1 constant_dynamic-slice_fusion.5
  14.3 0.4 convolution_add_fusion.2
  14.8 0.1 constant_dynamic-slice_fusion.5
  14.9 0.4 convolution_add_fusion.2
  15.3 0.1 copy.15
  15.5 0.5 fusion.9
  16.0 1.0 copy.16
  17.1 60.7 %all-gather.3.cloned.1.call-done = f32[640,79,9]{1,0,2:T(8,128)} async-done(((f32[80,79,9]{1,0,2:T(8,128)}), f32[640,79,9]{1,0,2:T(8,128)}) %all-gather.3.cloned.1.call-update) | async-done | bytes 1820176 | tf_op jit(solution)/shard_map/all_gather | solution.py:52
  77.8 2.1 %reduce_sum.9 = f32[80,79,9]{1,0,2:T(8,128)S(1)} reduce(f32[8,80,79,9]{2,1,0,3:T(8,128)} %bitcast.27, f32[]{:T(128)} %constant.53.clone.1), dimensions={0}, to_apply=%region_2.3 | reduce | flops 398160 | bytes 2047684 | tf_op jit(solution)/shard_map/reduce_sum | solution.py:52
  79.9 0.4 copy.18
  80.3 0.8 fusion.6
  81.1 1.3 %copy.19 = f32[80,2528]{1,0:T(8,128)} copy(f32[80,2528]{0,1:T(8,128)S(1)} %bitcast.25) | data formatting | bytes 1617920 | tf_op jit(solution)/shard_map/reshape | solution.py:57
  82.4 34.0 %all-reduce.2.cloned.1.call-done = f32[80,2528]{1,0:T(8,128)} async-done(((f32[80,2528]{1,0:T(8,128)}), f32[80,2528]{1,0:T(8,128)}) %all-reduce.2.cloned.1.call-update) | async-done | bytes 808976 | tf_op jit(solution)/shard_map/psum | solution.py:57
  116.4 1.2 broadcast_multiply_fusion
  117.6 0.9 fusion.15
  (17 shorter events, 0.2 us)
Async XLA Ops:
  7.2 70.7 %all-gather.3.cloned.1.call-start = ((), (), s32[]{:S(2)}) async-start(), calls=%async_computation.1 | async-start | bytes 3317760 | tf_op jit(solution)/shard_map/all_gather | solution.py:52
  17.0 99.4 %all-reduce.2.cloned.1.call-start = ((), (), s32[]{:S(2)}) async-start(), calls=%async_computation | async-start | bytes 1638400 | tf_op jit(solution)/shard_map/psum | solution.py:57
Sparse Core Ops, SparseCore 0:
  17.1 60.6 all-gather.2
  82.5 33.8 all-reduce.1
